TPU v7x, 32 devices: a whole 2x2x4 slice. The times are simulated.
32 devices in a mesh: band: 16 (over z, y, core), fft: 2 (over x).
Axes of the slice: x: 2, y: 2, z: 4, core: 2. Of those that a mesh axis runs over, the one named last changes fastest.
Arguments:
- coefficients: float32 [16, 2, 72, 5184], P('band', None, None, 'fft'), may hold values from -0.009765625 to 0.009765625
- col_index: int32 [5184], replicated, may hold values from 0 to 5183, each once
- occupation: int32 [16], P('band'), may hold values from 1 to 4
Outputs:
- density: float32 [288, 288, 288], P('band', 'fft')
Inputs may be any that keep to these rules, and one draw needn't show every extreme that they name: `col_index`: each number of the range appears once.
All inputs are finite; a program needn't handle non-finite values.
Results may differ from a plain program's by a relative error of at most 0.0003.
Values sent between devices are 32-bit elements; how exact they have to be, the bound alone decides.
A program may use at most 128 MiB of HBM per device.

v0:
```python
import math
import jax
import jax.numpy as jnp
from jax import lax
from jax.sharding import PartitionSpec as P

NC = 144
NF = 288
KZ = 72
NCOLS = 5184


def product(pattern, operand_a, operand_b):
    return jnp.einsum(pattern, operand_a, operand_b, precision=lax.Precision.HIGHEST)


def phase_tables(wave_count, offset, points):
    wave_index = jnp.arange(wave_count, dtype=jnp.int32) - offset
    grid_index = jnp.arange(points, dtype=jnp.int32)
    phases = jnp.mod(wave_index[:, None] * grid_index[None, :], points)
    angles = phases.astype(jnp.float32) * (2.0 * math.pi / points)
    return (jnp.cos(angles), jnp.sin(angles))


def interpolation_matrix(coarse_len, fine_len):
    fine_index = jnp.arange(fine_len, dtype=jnp.int32)
    coarse_index = jnp.arange(coarse_len, dtype=jnp.int32)
    wave_index = jnp.arange(1, coarse_len // 2, dtype=jnp.int32)
    offsets = fine_index[:, None] - 2 * coarse_index[None, :]
    phases = jnp.mod(offsets[:, :, None] * wave_index[None, None, :], fine_len)
    angles = phases.astype(jnp.float32) * (2.0 * math.pi / fine_len)
    return (1.0 + 2.0 * jnp.sum(jnp.cos(angles), axis=2)) / coarse_len


def rotate(pattern, real_part, imag_part, cos_table, sin_table):
    out_real = product(pattern, real_part, cos_table) - product(pattern, imag_part, sin_table)
    out_imag = product(pattern, real_part, sin_table) + product(pattern, imag_part, cos_table)
    return (out_real, out_imag)


def local(coefficients, col_index, occupation):
    band_here = coefficients.shape[0]
    col_count = coefficients.shape[3]
    band_total = band_here * lax.axis_size("band")
    radius = KZ // 2
    col_start = lax.axis_index("fft") * col_count
    local_cols = lax.dynamic_slice_in_dim(col_index, col_start, col_count)
    first_wave = local_cols // KZ - radius
    second_wave = local_cols % KZ - radius
    third_wave = jnp.arange(KZ, dtype=jnp.int32) - radius
    radial = (first_wave * first_wave + second_wave * second_wave)[None, :] + (
        third_wave * third_wave
    )[:, None]
    inside = (radial <= radius * radius).astype(jnp.float32)
    masked = coefficients * inside
    cos_table, sin_table = phase_tables(KZ, radius, NC)
    line_real, line_imag = rotate("bkc,kz->bzc", masked[:, 0], masked[:, 1], cos_table, sin_table)
    z_lines = jnp.stack([line_real, line_imag], axis=1)
    inverse = jnp.zeros((NCOLS,), jnp.int32).at[col_index].set(jnp.arange(NCOLS, dtype=jnp.int32))
    block_in = lax.all_to_all(z_lines, "fft", split_axis=2, concat_axis=3, tiled=True)
    box_grid = jnp.take(block_in, inverse, axis=3)
    box_grid = box_grid.reshape(block_in.shape[0], 2, block_in.shape[2], KZ, KZ)
    half_real, half_imag = rotate(
        "bzak,kr->bzar", box_grid[:, 0], box_grid[:, 1], cos_table, sin_table
    )
    full_real, full_imag = rotate("bzar,as->bzsr", half_real, half_imag, cos_table, sin_table)
    moduli = full_real * full_real + full_imag * full_imag
    weights = occupation.astype(jnp.float32) / band_total
    partial_value = product("b,bzxy->zxy", weights, moduli)
    interpolation = interpolation_matrix(NC, NF)
    row_share = NF // lax.axis_size("band")
    summed = lax.psum(partial_value, "band")
    own_rows = lax.dynamic_slice_in_dim(
        interpolation, lax.axis_index("band") * row_share, row_share, 0
    )
    reduced = product("zgb,fb->zgf", product("zab,ga->zgb", summed, own_rows), interpolation)
    return product(
        "rgf,hr->gfh",
        lax.all_to_all(reduced, "fft", split_axis=2, concat_axis=0, tiled=True),
        interpolation,
    )


def solution(mesh):
    return jax.shard_map(
        local,
        mesh=mesh,
        in_specs=(P("band", None, None, "fft"), P(), P("band")),
        out_specs=P("band", "fft", None),
        check_vma=False,
    )
```

profile of v0, /device:TPU:0, one launch (start us, length us, event | category | flops | bytes accessed | tf_op | source)
XLA Modules:
  0.0 451.8 jit_solution(9786847167849780601)
XLA Ops:
  7.5 1.6 broadcast_multiply_fusion
  9.1 1.6 fusion.18
  10.7 1.6 fusion.19
  12.4 1.7 fusion.8
  14.1 1.7 fusion.7
  16.0 3.2 copy.44
  19.3 4.2 all-to-all-start
  23.5 36.3 %scatter_custom_fusion = s32[5184]{0:T(1024)S(1)} fusion(s32[5184]{0:T(1024)S(1)} %compare_select_fusion.1, s32[5184]{0:T(1024)S(1)} %iota.59, s32[]{:T(128)} %constant.53.clone.1), kind=kCustom, calls=%fused_computation.112 | custom fusion | bytes 20740 | tf_op jit(solution)/shard_map/scatter | solution.py:59
  60.6 6.9 %copy.62 = f32[1,2,72,2,2592]{2,1,4,3,0:T(2,128)} copy(f32[1,2,72,2,2592]{4,1,2,3,0:T(2,128)S(1)} %bitcast.89) | data formatting | bytes 5971968 | tf_op jit(solution)/shard_map/all_to_all | solution.py:60
  67.5 19.1 %gather_fusion = f32[5184,2,72]{2,1,0:T(2,128)} fusion(f32[2,72,5184]{1,0,2:T(2,128)} %bitcast.87, s32[6144]{0:T(1024)S(1)} %pad_clamp_fusion), kind=kCustom, calls=%fused_computation | custom fusion | bytes 5992704 | tf_op jit(solution)/shard_map/jit(_take)/gather | solution.py:61
  86.6 8.5 %copy.63 = f32[1,2,72,72,72]{4,3,2,1,0:T(8,128)} copy(f32[1,2,72,72,72]{2,1,4,3,0:T(2,128)} %bitcast.88) | data formatting | bytes 5971968 | tf_op jit(solution)/shard_map/jit(_take)/gather | solution.py:61
  95.0 2.9 broadcast_select_fusion
  97.9 4.8 %fusion.10 = f32[72,72,144]{2,1,0:T(8,128)S(1)} fusion(f32[1,2,72,72,72]{4,3,2,1,0:T(8,128)S(1)} %broadcast_select_fusion, s32[72]{0:T(128)S(1)} %iota_add_fusion), kind=kOutput, calls=%fused_computation.22 | convolution fusion | flops 645065856 | bytes 5640704 | tf_op jit(solution)/shard_map/bzak,kr->bzar/dot_general | solution.py:14
  102.7 4.8 %fusion.13 = f32[72,72,144]{2,1,0:T(8,128)S(1)} fusion(f32[72,72,144]{2,1,0:T(8,128)S(1)} %fusion.10, f32[1,2,72,72,72]{4,3,2,1,0:T(8,128)S(1)} %broadcast_select_fusion, s32[72]{0:T(128)S(1)} %iota_add_fusion), kind=kOutput, calls=%fused_computation.25 | convolution fusion | flops 645812352 | bytes 10949120 | tf_op jit(solution)/shard_map/bzak,kr->bzar/dot_general | solution.py:14
  107.5 11.8 %fusion.26 = f32[144,72,144]{2,0,1:T(8,128)} fusion(f32[72,72,144]{2,1,0:T(8,128)S(1)} %fusion.13, s32[72]{0:T(128)S(1)} %iota_add_fusion), kind=kOutput, calls=%fused_computation.46 | convolution fusion | flops 1290038400 | bytes 8958240 | tf_op jit(solution)/shard_map/bzar,as->bzsr/dot_general | solution.py:14
  119.3 12.0 %fusion.34 = f32[144,72,144]{2,0,1:T(8,128)} fusion(f32[72,72,144]{2,1,0:T(8,128)S(1)} %fusion.13, s32[72]{0:T(128)S(1)} %iota_add_fusion), kind=kOutput, calls=%fused_computation.54 | convolution fusion | flops 1290038400 | bytes 8958240 | tf_op jit(solution)/shard_map/bzar,as->bzsr/dot_general | solution.py:14
  131.3 4.8 %fusion.9 = f32[72,72,144]{2,1,0:T(8,128)S(1)} fusion(f32[1,2,72,72,72]{4,3,2,1,0:T(8,128)S(1)} %broadcast_select_fusion, s32[72]{0:T(128)S(1)} %iota_add_fusion), kind=kOutput, calls=%fused_computation.21 | convolution fusion | flops 645065856 | bytes 5640704 | tf_op jit(solution)/shard_map/bzak,kr->bzar/dot_general | solution.py:14
  136.1 4.8 %fusion.14 = f32[72,72,144]{2,1,0:T(8,128)S(1)} fusion(f32[72,72,144]{2,1,0:T(8,128)S(1)} %fusion.9, f32[1,2,72,72,72]{4,3,2,1,0:T(8,128)S(1)} %broadcast_select_fusion, s32[72]{0:T(128)S(1)} %iota_add_fusion), kind=kOutput, calls=%fused_computation.26 | convolution fusion | flops 645812352 | bytes 10949120 | tf_op jit(solution)/shard_map/bzak,kr->bzar/dot_general | solution.py:14
  140.9 11.7 %fusion.28 = f32[144,72,144]{2,0,1:T(8,128)} fusion(f32[72,72,144]{2,1,0:T(8,128)S(1)} %fusion.14, s32[72]{0:T(128)S(1)} %iota_add_fusion), kind=kOutput, calls=%fused_computation.48 | convolution fusion | flops 1290038400 | bytes 8958240 | tf_op jit(solution)/shard_map/bzar,as->bzsr/dot_general | solution.py:14
  152.6 21.9 %multiply_bitcast_fusion = f32[72,144,144]{2,1,0:T(8,128)} fusion(f32[144,72,144]{2,0,1:T(8,128)} %fusion.26, f32[144,72,144]{2,0,1:T(8,128)} %fusion.34, f32[144,72,144]{2,0,1:T(8,128)} %fusion.28, f32[]{:T(128)} %bitcast.1, f32[72,72,144]{2,1,0:T(8,128)} %copy-done, s32[72]{0:T(128)S(1)} %iota_add_fusion), kind=kOutput, calls=%fused_computation.11 | convolution fusion | flops 1298996352 | bytes 26874148 | tf_op jit(solution)/shard_map/bzar,as->bzsr/dot_general | solution.py:14
  174.6 61.2 %fusion.3 = f32[288,144]{0,1:T(8,128)S(1)} fusion(s32[71]{0:T(128)S(1)} %iota_add_fusion.1, s32[288,144]{0,1:T(8,128)S(1)} %iota_subtract_fusion), kind=kLoop, calls=%fused_computation.6 | loop fusion | flops 29403648 | bytes 332060 | tf_op jit(solution)/shard_map/reduce_sum | solution.py:32
  235.9 144.0 %all-reduce.2.cloned.1.call-done = f32[72,144,144]{2,1,0:T(8,128)} async-done(((f32[72,144,144]{2,1,0:T(8,128)}), f32[72,144,144]{2,1,0:T(8,128)}) %all-reduce.2.cloned.1.call-update) | async-done | bytes 5971984 | tf_op jit(solution)/shard_map/psum | solution.py:72
  379.9 8.3 %convolution_bitcast_fusion = f32[72,18,144]{2,1,0:T(8,128)S(1)} fusion(f32[72,144,144]{2,1,0:T(8,128)} %all-reduce.2.cloned.1.call-done, f32[288,144]{0,1:T(8,128)S(1)} %add_multiply_fusion, s32[]{:T(128)S(6)} %select_n.74), kind=kOutput, calls=%fused_computation.27 | convolution fusion | flops 322486272 | bytes 6792196 | tf_op jit(solution)/shard_map/zab,ga->zgb/dot_general | solution.py:14
  388.2 3.8 fusion.15
  392.0 3.5 copy.54
  395.5 3.8 reshape.191
  399.2 22.0 %all_to_all.36 = f32[2,1,186624]{2,1,0:T(1,128)S(1)} all-to-all(f32[2,1,186624]{2,1,0:T(1,128)} %reshape.191), channel_id=1, replica_groups=mesh['band'=16,'fft'=2] {'fft'}, dimensions={0} | all-to-all | bytes 2985984 | tf_op jit(solution)/shard_map/all_to_all | solution.py:79
  421.8 6.2 %reduce = f32[2,186624]{1,0:T(2,128)} reduce(f32[2,1,186624]{2,1,0:T(1,128)S(1)} %all_to_all.36, f32[]{:T(128)} %broadcast.120), dimensions={1}, to_apply=%all_to_all.30.reduce_sub_computation | reduce | bytes 2985988 | tf_op jit(solution)/shard_map/all_to_all | solution.py:79
  428.0 4.1 reshape.192
  432.1 3.6 copy.72
  435.7 3.3 all_to_all.33
  439.0 5.8 %fusion.20 = f32[18,144,288]{2,1,0:T(8,128)} fusion(f32[144,18,144]{0,2,1:T(8,128)S(1)} %all_to_all.33, f32[288,144]{0,1:T(8,128)S(1)} %copy-done.2), kind=kOutput, calls=%fused_computation.37 | convolution fusion | flops 1290069504 | bytes 4644864 | tf_op jit(solution)/shard_map/rgf,hr->gfh/dot_general | solution.py:14
  (27 shorter events, 2.1 us)
Async XLA Ops:
  16.0 7.5 %copy-start.3 = (s32[5184]{0:T(1024)S(1)}, s32[5184]{0:T(1024)}, u32[]{:S(2)}) copy-start(s32[5184]{0:T(1024)} %param.4) | copy-start | bytes 62212
  19.3 41.3 %all-to-all-start = ((f32[1,2,144,2592]{3,1,0,2:T(2,128)}), f32[1,2,144,2592]{3,1,0,2:T(2,128)S(1)}, u32[]{:S(2)}, u32[]{:S(2)}) async-start(f32[1,2,144,2592]{3,1,0,2:T(2,128)} %copy.44), calls=%async_computation | async-start | bytes 6193152 | tf_op jit(solution)/shard_map/all_to_all | solution.py:60
  23.5 356.4 %all-reduce.2.cloned.1.call-start = ((), (), s32[]{:S(2)}) async-start(), calls=%async_computation.2 | async-start | bytes 21233664 | tf_op jit(solution)/shard_map/psum | solution.py:72
  140.9 11.7 %copy-start = (f32[72,72,144]{2,1,0:T(8,128)}, f32[72,72,144]{2,1,0:T(8,128)S(1)}, u32[]{:S(2)}) copy-start(f32[72,72,144]{2,1,0:T(8,128)S(1)} %fusion.14) | copy-start | bytes 8957956
  235.8 152.3 %copy-start.1 = (f32[288,144]{0,1:T(8,128)}, f32[288,144]{0,1:T(8,128)S(1)}, u32[]{:S(2)}) copy-start(f32[288,144]{0,1:T(8,128)S(1)} %fusion.3) | copy-start | bytes 497668
  435.7 3.3 copy-start.2
Sparse Core Ops, SparseCore 0:
  174.6 205.2 all-reduce.1
where the time goes:
time: 460 us; the launch traced here: 452 us
  waiting for transfers between devices  144 us (31%)
  matrix products  101 us (22%)
  local copies, waits for them, and re-layouts  92.8 us (20%)
  other arithmetic  73.2 us (16%)
  blocking collectives  22 us (5%)
  between operations  14.5 us (3%)
    psum x1, waiting for transfers between devices, local(): summed = lax.psum(partial_value, 'band')  144 us
    dot_general x15, matrix products, product(): jnp.einsum(pattern, operand_a, operand_b, precision=lax.Precision.HIGHEST)  101 us
    reduce_sum x1, other arithmetic, interpolation_matrix(): return (1.0 + 2.0 * jnp.sum(jnp.cos(angles), axis=2)) / coarse_len  61.2 us
    scatter x1, local copies, waits for them, and re-layouts, local(): jnp.zeros((NCOLS,), jnp.int32).at[col_index]  36.3 us
    gather x2, local copies, waits for them, and re-layouts, local(): box_grid = jnp.take(block_in, inverse, axis=3)  27.5 us
    all_to_all x1, blocking collectives, local(): lax.all_to_all(reduced, 'fft', split_axis=2, concat_axis=0, tiled=True)  22 us
  transfers between devices with their start and end apart: 2, of which 1 were waited for; matrix products, arithmetic and copies ran while one was open for 22% of the time, Pallas kernels for 0%

commit v1 on v0

--- a/solution.py
+++ b/solution.py
@@ -76,7 +76,12 @@
     reduced = product("zgb,fb->zgf", product("zab,ga->zgb", summed, own_rows), interpolation)
     return product(
         "rgf,hr->gfh",
-        lax.all_to_all(reduced, "fft", split_axis=2, concat_axis=0, tiled=True),
+        jnp.concatenate(
+            lax.all_to_all(
+                jnp.stack(jnp.split(reduced, lax.axis_size("fft"), axis=2)), "fft", 0, 0
+            ),
+            axis=0,
+        ),
         interpolation,
     )
 

time: 460 us -> 444 us (0.965)
  local copies, waits for them, and re-layouts: 92.8 us -> 64.3 us
  blocking collectives: 22 us -> 33.4 us
  waiting for transfers between devices: 144 us -> 152 us
  other arithmetic: 73.2 us -> 67.2 us
    all_to_all x1, blocking collectives: 22 us -> 33.4 us  [local(): lax.all_to_all(jnp.stack(jnp.split(reduced, lax.axis_size('fft'), axis=2)...]
    scatter x1, local copies, waits for them, and re-layouts: 36.3 us -> 25.7 us  [local(): jnp.zeros((NCOLS,), jnp.int32).at[col_index]]
    all_to_all x1, waiting for transfers between devices: 0.01 us -> 10.1 us  [local(): lax.all_to_all(z_lines, 'fft', split_axis=2, concat_axis=3, tiled=True)]
    unnamed x10 -> x4, local copies, waits for them, and re-layouts: 7.84 us -> 0.01 us
    all_to_all x3 -> x1, local copies, waits for them, and re-layouts: 7.45 us -> 0.34 us  [local(): lax.all_to_all(jnp.stack(jnp.split(reduced, lax.axis_size('fft'), axis=2)...]
    all_to_all x1 -> x0, other arithmetic: 6.22 us -> none  [local(): lax.all_to_all(reduced, 'fft', split_axis=2, concat_axis=0, tiled=True)]
  transfers between devices with their start and end apart: 2 -> 2, of which waited for: 1 -> 2; matrix products, arithmetic and copies ran while one was open for 22% -> 20% of each run, Pallas kernels for 0% -> 0%
where the time goes in v1:
time: 444 us; the launch traced here: 437 us
  waiting for transfers between devices  152 us (34%)
  matrix products  101 us (23%)
  other arithmetic  67.2 us (15%)
  local copies, waits for them, and re-layouts  64.3 us (14%)
  blocking collectives  33.4 us (8%)
  between operations  14.5 us (3%)
    psum x1, waiting for transfers between devices, local(): summed = lax.psum(partial_value, 'band')  142 us
    dot_general x15, matrix products, product(): jnp.einsum(pattern, operand_a, operand_b, precision=lax.Precision.HIGHEST)  101 us
    reduce_sum x1, other arithmetic, interpolation_matrix(): return (1.0 + 2.0 * jnp.sum(jnp.cos(angles), axis=2)) / coarse_len  61.2 us
    all_to_all x1, blocking collectives, local(): lax.all_to_all(jnp.stack(jnp.split(reduced, lax.axis_size('fft'), axis=2)...  33.4 us
    gather x2, local copies, waits for them, and re-layouts, local(): box_grid = jnp.take(block_in, inverse, axis=3)  27.5 us
    scatter x1, local copies, waits for them, and re-layouts, local(): jnp.zeros((NCOLS,), jnp.int32).at[col_index]  25.7 us
    all_to_all x1, waiting for transfers between devices, local(): lax.all_to_all(z_lines, 'fft', split_axis=2, concat_axis=3, tiled=True)  10.1 us
  transfers between devices with their start and end apart: 2, of which 2 were waited for; matrix products, arithmetic and copies ran while one was open for 20% of the time, Pallas kernels for 0%

profile of v1, /device:TPU:0, one launch (start us, length us, event | category | flops | bytes accessed | tf_op | source)
XLA Modules:
  0.0 436.8 jit_solution(9423977052583883542)
XLA Ops:
  6.5 0.8 fusion.105
  7.5 1.6 broadcast_multiply_fusion
  9.1 1.6 fusion.18
  10.7 1.6 fusion.19
  12.4 1.7 fusion.8
  14.1 1.7 fusion.7
  15.8 0.2 pad_maximum_fusion
  16.1 3.2 copy.44
  19.3 4.2 all-to-all-start
  23.5 25.7 %scatter_custom_fusion = s32[5184]{0:T(1024)S(1)} fusion(s32[5184]{0:T(1024)S(1)} %compare_select_fusion.1, s32[5184]{0:T(1024)S(1)} %iota.59, s32[]{:T(128)} %constant.53.clone.1), kind=kCustom, calls=%fused_computation.114 | custom fusion | bytes 20740 | tf_op jit(solution)/shard_map/scatter | solution.py:59
  50.1 10.1 %all-to-all-done = f32[1,2,144,2592]{3,1,0,2:T(2,128)S(1)} async-done(((f32[1,2,144,2592]{3,1,0,2:T(2,128)}), f32[1,2,144,2592]{3,1,0,2:T(2,128)S(1)}, u32[]{:S(2)}, u32[]{:S(2)}) %all-to-all-start) | async-done | bytes 2986016 | tf_op jit(solution)/shard_map/all_to_all | solution.py:60
  60.3 6.9 %copy.63 = f32[1,2,72,2,2592]{2,1,4,3,0:T(2,128)} copy(f32[1,2,72,2,2592]{4,1,2,3,0:T(2,128)S(1)} %bitcast.84) | data formatting | bytes 5971968 | tf_op jit(solution)/shard_map/all_to_all | solution.py:60
  67.2 19.1 %gather_fusion = f32[5184,2,72]{2,1,0:T(2,128)} fusion(f32[2,72,5184]{1,0,2:T(2,128)} %bitcast.82, s32[6144]{0:T(1024)S(1)} %pad_clamp_fusion), kind=kCustom, calls=%fused_computation | custom fusion | bytes 5992704 | tf_op jit(solution)/shard_map/jit(_take)/gather | solution.py:61
  86.2 8.5 %copy.64 = f32[1,2,72,72,72]{4,3,2,1,0:T(8,128)} copy(f32[1,2,72,72,72]{2,1,4,3,0:T(2,128)} %bitcast.83) | data formatting | bytes 5971968 | tf_op jit(solution)/shard_map/jit(_take)/gather | solution.py:61
  94.7 2.9 broadcast_select_fusion
  97.6 4.8 %fusion.10 = f32[72,72,144]{2,1,0:T(8,128)S(1)} fusion(f32[1,2,72,72,72]{4,3,2,1,0:T(8,128)S(1)} %broadcast_select_fusion, s32[72]{0:T(128)S(1)} %iota_add_fusion), kind=kOutput, calls=%fused_computation.22 | convolution fusion | flops 645065856 | bytes 5640704 | tf_op jit(solution)/shard_map/bzak,kr->bzar/dot_general | solution.py:14
  102.4 4.8 %fusion.13 = f32[72,72,144]{2,1,0:T(8,128)S(1)} fusion(f32[72,72,144]{2,1,0:T(8,128)S(1)} %fusion.10, f32[1,2,72,72,72]{4,3,2,1,0:T(8,128)S(1)} %broadcast_select_fusion, s32[72]{0:T(128)S(1)} %iota_add_fusion), kind=kOutput, calls=%fused_computation.25 | convolution fusion | flops 645812352 | bytes 10949120 | tf_op jit(solution)/shard_map/bzak,kr->bzar/dot_general | solution.py:14
  107.2 11.8 %fusion.26 = f32[144,72,144]{2,0,1:T(8,128)} fusion(f32[72,72,144]{2,1,0:T(8,128)S(1)} %fusion.13, s32[72]{0:T(128)S(1)} %iota_add_fusion), kind=kOutput, calls=%fused_computation.48 | convolution fusion | flops 1290038400 | bytes 8958240 | tf_op jit(solution)/shard_map/bzar,as->bzsr/dot_general | solution.py:14
  118.9 11.8 %fusion.34 = f32[144,72,144]{2,0,1:T(8,128)} fusion(f32[72,72,144]{2,1,0:T(8,128)S(1)} %fusion.13, s32[72]{0:T(128)S(1)} %iota_add_fusion), kind=kOutput, calls=%fused_computation.56 | convolution fusion | flops 1290038400 | bytes 8958240 | tf_op jit(solution)/shard_map/bzar,as->bzsr/dot_general | solution.py:14
  130.8 4.8 %fusion.9 = f32[72,72,144]{2,1,0:T(8,128)S(1)} fusion(f32[1,2,72,72,72]{4,3,2,1,0:T(8,128)S(1)} %broadcast_select_fusion, s32[72]{0:T(128)S(1)} %iota_add_fusion), kind=kOutput, calls=%fused_computation.21 | convolution fusion | flops 645065856 | bytes 5640704 | tf_op jit(solution)/shard_map/bzak,kr->bzar/dot_general | solution.py:14
  135.5 4.8 %fusion.14 = f32[72,72,144]{2,1,0:T(8,128)S(1)} fusion(f32[72,72,144]{2,1,0:T(8,128)S(1)} %fusion.9, f32[1,2,72,72,72]{4,3,2,1,0:T(8,128)S(1)} %broadcast_select_fusion, s32[72]{0:T(128)S(1)} %iota_add_fusion), kind=kOutput, calls=%fused_computation.26 | convolution fusion | flops 645812352 | bytes 10949120 | tf_op jit(solution)/shard_map/bzak,kr->bzar/dot_general | solution.py:14
  140.3 11.9 %fusion.28 = f32[144,72,144]{2,0,1:T(8,128)} fusion(f32[72,72,144]{2,1,0:T(8,128)S(1)} %fusion.14, s32[72]{0:T(128)S(1)} %iota_add_fusion), kind=kOutput, calls=%fused_computation.50 | convolution fusion | flops 1290038400 | bytes 8958240 | tf_op jit(solution)/shard_map/bzar,as->bzsr/dot_general | solution.py:14
  152.3 21.6 %multiply_bitcast_fusion = f32[72,144,144]{2,1,0:T(8,128)} fusion(f32[144,72,144]{2,0,1:T(8,128)} %fusion.26, f32[144,72,144]{2,0,1:T(8,128)} %fusion.34, f32[144,72,144]{2,0,1:T(8,128)} %fusion.28, f32[]{:T(128)} %bitcast.1, f32[72,72,144]{2,1,0:T(8,128)} %copy-done, s32[72]{0:T(128)S(1)} %iota_add_fusion), kind=kOutput, calls=%fused_computation.11 | convolution fusion | flops 1298996352 | bytes 26874148 | tf_op jit(solution)/shard_map/bzar,as->bzsr/dot_general | solution.py:14
  174.0 61.2 %fusion.3 = f32[288,144]{0,1:T(8,128)S(1)} fusion(s32[71]{0:T(128)S(1)} %iota_add_fusion.1, s32[288,144]{0,1:T(8,128)S(1)} %iota_subtract_fusion), kind=kLoop, calls=%fused_computation.6 | loop fusion | flops 29403648 | bytes 332060 | tf_op jit(solution)/shard_map/reduce_sum | solution.py:32
  235.2 141.7 %all-reduce.2.cloned.1.call-done = f32[72,144,144]{2,1,0:T(8,128)} async-done(((f32[72,144,144]{2,1,0:T(8,128)}), f32[72,144,144]{2,1,0:T(8,128)}) %all-reduce.2.cloned.1.call-update) | async-done | bytes 5971984 | tf_op jit(solution)/shard_map/psum | solution.py:72
  376.9 8.1 %convolution_bitcast_fusion = f32[72,18,144]{2,1,0:T(8,128)S(1)} fusion(f32[72,144,144]{2,1,0:T(8,128)} %all-reduce.2.cloned.1.call-done, f32[288,144]{0,1:T(8,128)S(1)} %add_multiply_fusion, s32[]{:T(128)S(6)} %select_n.74), kind=kOutput, calls=%fused_computation.27 | convolution fusion | flops 322486272 | bytes 6792196 | tf_op jit(solution)/shard_map/zab,ga->zgb/dot_general | solution.py:14
  385.0 2.6 fusion.15
  387.6 0.4 slice_bitcast_fusion.11
  388.0 0.2 pad_maximum_fusion.1
  388.2 33.4 %all_to_all.23 = f32[2,72,18,144]{3,1,2,0:T(8,128)S(1)} all-to-all(f32[2,72,18,144]{3,1,2,0:T(8,128)S(1)} %pad_maximum_fusion.1), channel_id=1, replica_groups=mesh['band'=16,'fft'=2] {'fft'}, dimensions={0} | all-to-all | bytes 2985984 | tf_op jit(solution)/shard_map/all_to_all | solution.py:80
  421.6 0.3 copy.54
  422.0 7.7 %fusion.20 = f32[18,144,288]{2,1,0:T(8,128)} fusion(f32[144,18,144]{2,0,1:T(8,128)S(1)} %bitcast.85, f32[288,144]{0,1:T(8,128)S(1)} %fusion.3), kind=kOutput, calls=%fused_computation.39 | convolution fusion | flops 1290069504 | bytes 4644864 | tf_op jit(solution)/shard_map/rgf,hr->gfh/dot_general | solution.py:14
  (19 shorter events, 0.4 us)
Async XLA Ops:
  16.0 7.5 %copy-start.1 = (s32[5184]{0:T(1024)S(1)}, s32[5184]{0:T(1024)}, u32[]{:S(2)}) copy-start(s32[5184]{0:T(1024)} %param.4) | copy-start | bytes 62212
  19.3 41.0 %all-to-all-start = ((f32[1,2,144,2592]{3,1,0,2:T(2,128)}), f32[1,2,144,2592]{3,1,0,2:T(2,128)S(1)}, u32[]{:S(2)}, u32[]{:S(2)}) async-start(f32[1,2,144,2592]{3,1,0,2:T(2,128)} %copy.44), calls=%async_computation | async-start | bytes 6193152 | tf_op jit(solution)/shard_map/all_to_all | solution.py:60
  23.5 353.4 %all-reduce.2.cloned.1.call-start = ((), (), s32[]{:S(2)}) async-start(), calls=%async_computation.2 | async-start | bytes 21233664 | tf_op jit(solution)/shard_map/psum | solution.py:72
  140.3 11.9 %copy-start = (f32[72,72,144]{2,1,0:T(8,128)}, f32[72,72,144]{2,1,0:T(8,128)S(1)}, u32[]{:S(2)}) copy-start(f32[72,72,144]{2,1,0:T(8,128)S(1)} %fusion.14) | copy-start | bytes 8957956
Sparse Core Ops, SparseCore 0:
  174.0 202.8 all-reduce.1
